TPU v7x, 8 devices: a whole 2x2x1 slice. The times are simulated.
8 devices in a mesh: frag: 1 (over z), dev: 8 (over y, x, core).
Axes of the slice: x: 2, y: 2, z: 1, core: 2. Of those that a mesh axis runs over, the one named last changes fastest.
Arguments:
- ao_ints: bfloat16 [152, 152, 152, 152], P(('frag', 'dev'))
- occ_coef: bfloat16 [152, 33], P('frag')
- virt_coef: bfloat16 [152, 104], P('frag')
Outputs:
- output: float32 [33, 104, 3432], P('frag', None, 'dev')
All inputs are finite; a program needn't handle non-finite values.
Results may differ from a plain program's by a relative error of at most 0.001.
Values are sent between devices in bfloat16 or wider.
A program may use at most 1 GiB of HBM per device.

v0:
```python
import jax
import jax.numpy as jnp
from jax import lax
from jax.sharding import PartitionSpec as P


def solution(mesh):
    def local_part(ao_rows, occ_coef, virt_coef):
        quarter = jnp.einsum("pqrs,rj->pqsj", ao_rows, occ_coef, preferred_element_type=jnp.float32).astype(jnp.bfloat16)
        half_ints = jnp.einsum("pqsj,sb->pqjb", quarter, virt_coef, preferred_element_type=jnp.float32).astype(jnp.bfloat16)
        rows_here, ao_dim, occ_dim, virt_dim = half_ints.shape
        half_ints = half_ints.reshape(rows_here, ao_dim, occ_dim * virt_dim)
        pair_block = lax.all_to_all(half_ints, "dev", 2, 0, tiled=True)
        three_quarter = jnp.einsum("qa,pqc->apc", virt_coef, pair_block, preferred_element_type=jnp.float32).astype(jnp.bfloat16)
        return jnp.einsum("pi,apc->iac", occ_coef, three_quarter, preferred_element_type=jnp.float32)

    return jax.shard_map(
        local_part,
        mesh=mesh,
        in_specs=(P(("frag", "dev"), None, None, None), P("frag", None), P("frag", None)),
        out_specs=P("frag", None, "dev"),
        check_vma=False,
    )
```

profile of v0, /device:TPU:0, one launch (start us, length us, event | category | flops | bytes accessed | tf_op | source)
XLA Modules:
  0.0 665.9 jit_solution(1278201484315855870)
XLA Ops:
  0.0 0.0 copy-start
  0.0 88.0 %convolution_convert_fusion = bf16[19,152,152,33]{2,3,1,0:T(8,128)(2,1)} fusion(bf16[19,152,152,152]{3,2,1,0:T(8,128)(2,1)} %param.3, bf16[152,33]{0,1:T(8,128)(2,1)} %param.4), kind=kOutput, calls=%fused_computation.2 | convolution fusion | flops 4418293248 | bytes 162431152 | tf_op jit(solution)/shard_map/pqrs,rj->pqsj/dot_general | solution.py:9
  88.0 0.0 copy-done
  88.0 34.2 %fusion.4 = bf16[19,152,33,104]{3,1,2,0:T(8,128)(2,1)} fusion(bf16[19,152,152,33]{2,3,1,0:T(8,128)(2,1)} %convolution_convert_fusion, bf16[152,104]{1,0:T(8,128)(2,1)S(1)} %copy-done), kind=kOutput, calls=%fused_computation.6 | convolution fusion | flops 3023042816 | bytes 48827264 | tf_op jit(solution)/shard_map/pqsj,sb->pqjb/dot_general | solution.py:10
  122.2 51.0 %copy.22 = bf16[19,152,33,104]{1,0,3,2:T(8,128)(2,1)} copy(bf16[19,152,33,104]{3,1,2,0:T(8,128)(2,1)} %fusion.4) | data formatting | bytes 39646464 | tf_op jit(solution)/shard_map/reshape | solution.py:12
  173.2 90.1 %reshape.8 = bf16[8,2,619476]{2,1,0:T(2,128)(2,1)} reshape(bf16[3432,19,152]{2,1,0:T(8,128)(2,1)} %bitcast.30) | data formatting | bytes 39646464
  263.3 224.7 %all_to_all.18 = bf16[8,2,619476]{2,1,0:T(2,128)(2,1)} all-to-all(bf16[8,2,619476]{2,1,0:T(2,128)(2,1)} %reshape.8), channel_id=1, replica_groups=mesh['frag'=1,'dev'=8] {'dev'}, dimensions={0} | all-to-all | bytes 39646464 | tf_op jit(solution)/shard_map/all_to_all | solution.py:13
  488.0 91.1 %reshape.9 = bf16[3432,19,152]{2,1,0:T(8,128)(2,1)} reshape(bf16[8,2,619476]{2,1,0:T(2,128)(2,1)} %all_to_all.18) | data formatting | bytes 39646464
  579.0 55.5 %copy.17 = bf16[8,19,152,429]{3,2,1,0:T(8,128)(2,1)} copy(bf16[8,19,152,429]{2,1,3,0:T(8,128)(2,1)} %bitcast.31) | data formatting | bytes 39646464 | tf_op jit(solution)/shard_map/all_to_all | solution.py:13
  634.5 0.0 copy-start.1
  634.5 13.5 %convert_bitcast_fusion = bf16[104,152,429]{2,0,1:T(8,128)(2,1)} fusion(bf16[152,152,429]{2,1,0:T(8,128)(2,1)} %bitcast.32, bf16[152,104]{1,0:T(8,128)(2,1)S(1)} %copy-done), kind=kOutput, calls=%fused_computation.5 | convolution fusion | flops 2068397824 | bytes 33418112 | tf_op jit(solution)/shard_map/qa,pqc->apc/dot_general | solution.py:14
  648.0 0.0 copy-done.1
  648.0 10.9 %fusion.7 = f32[33,104,429]{2,0,1:T(8,128)S(1)} fusion(bf16[104,152,429]{2,0,1:T(8,128)(2,1)} %convert_bitcast_fusion, bf16[152,33]{0,1:T(8,128)(2,1)S(1)} %copy-done.1), kind=kOutput, calls=%fused_computation.7 | convolution fusion | flops 447587712 | bytes 19462608 | tf_op jit(solution)/shard_map/pi,apc->iac/dot_general | solution.py:15
  658.9 7.0 %copy.19 = f32[33,104,429]{2,1,0:T(8,128)} copy(f32[33,104,429]{2,0,1:T(8,128)S(1)} %fusion.7) | data formatting | bytes 11778624 | tf_op jit(solution)/shard_map/pi,apc->iac/dot_general | solution.py:15
Async XLA Ops:
  0.0 88.0 %copy-start = (bf16[152,104]{1,0:T(8,128)(2,1)S(1)}, bf16[152,104]{1,0:T(8,128)(2,1)}, u32[]{:S(2)}) copy-start(bf16[152,104]{1,0:T(8,128)(2,1)} %param.5) | copy-start | bytes 94852
  634.5 13.5 %copy-start.1 = (bf16[152,33]{0,1:T(8,128)(2,1)S(1)}, bf16[152,33]{0,1:T(8,128)(2,1)}, u32[]{:S(2)}) copy-start(bf16[152,33]{0,1:T(8,128)(2,1)} %param.4) | copy-start | bytes 30100
where the time goes:
time: 670 us; the launch traced here: 666 us
  local copies, waits for them, and re-layouts  295 us (44%)
  blocking collectives  225 us (34%)
  matrix products  147 us (22%)
    all_to_all x1, blocking collectives, local_part(): pair_block = lax.all_to_all(half_ints, 'dev', 2, 0, tiled=True)  225 us
    unnamed x6, local copies, waits for them, and re-layouts  181 us
    dot_general x1, matrix products, local_part(): jnp.einsum('pqrs,rj->pqsj', ao_rows, occ_coef, preferred_element_type=jnp...  88 us
    all_to_all x1, local copies, waits for them, and re-layouts, local_part(): pair_block = lax.all_to_all(half_ints, 'dev', 2, 0, tiled=True)  55.5 us
    reshape x1, local copies, waits for them, and re-layouts, local_part(): half_ints = half_ints.reshape(rows_here, ao_dim, occ_dim * virt_dim)  51 us
    dot_general x1, matrix products, local_part(): jnp.einsum('pqsj,sb->pqjb', quarter, virt_coef, preferred_element_type=jn...  34.2 us
    dot_general x1, matrix products, local_part(): jnp.einsum('qa,pqc->apc', virt_coef, pair_block, preferred_element_type=j...  13.5 us

commit v1 on v0

v1 whole, which is shorter than its diff:
```python
import functools

import jax
import jax.numpy as jnp
from jax import lax
from jax.experimental import pallas as pl
from jax.experimental.pallas import tpu as pltpu
from jax.sharding import PartitionSpec as P

F32 = jnp.float32
BF16 = jnp.bfloat16
AO, OCC, VIRT = 152, 33, 104
DEVS = 8
ROWS = AO // DEVS
PAIRS = OCC * VIRT // DEVS
PITCH = 40
CHUNK = 19
CHUNKS = AO // CHUNK
SLOTS = 8
BLK = 3 * VIRT + 56
LANES = 128


def _exchange_kernel(a_hbm, cot_ref, cv_ref, g_out, abuf, cot, cvp, cvt, ts0, ts1, gsend, asem, ssem, rsem, lsem):
    me = lax.axis_index("dev")

    def a_copy(n):
        return pltpu.make_async_copy(
            a_hbm.at[n // CHUNKS, pl.ds(lax.rem(n, CHUNKS) * CHUNK, CHUNK)],
            abuf.at[lax.rem(n, SLOTS)],
            asem.at[lax.rem(n, SLOTS)],
        )

    for n in range(SLOTS):
        a_copy(n).start()

    barrier = pltpu.get_barrier_semaphore()
    for k in range(1, DEVS):
        pl.semaphore_signal(
            barrier, inc=1, device_id={"dev": lax.rem(me + k, DEVS)}, device_id_type=pl.DeviceIdType.MESH
        )

    cot[...] = jnp.zeros_like(cot)
    cot[0:OCC, :] = cot_ref[...]
    cvp[...] = jnp.zeros_like(cvp)
    cvp[0:AO, 0:VIRT] = cv_ref[...]
    cvt[...] = cvp[...].astype(F32).T[0:VIRT, :].astype(BF16)
    ts1[...] = jnp.zeros_like(ts1)

    pl.semaphore_wait(barrier, DEVS - 1)

    lane = lax.broadcasted_iota(jnp.int32, (VIRT, LANES), 1)
    lane56 = lax.broadcasted_iota(jnp.int32, (56, LANES), 1)

    def send(row, d):
        @pl.when(d != me)
        def _():
            pltpu.make_async_remote_copy(
                src_ref=gsend.at[row, d],
                dst_ref=g_out.at[me * ROWS + row],
                send_sem=ssem.at[row, d],
                recv_sem=rsem.at[row, me],
                device_id={"dev": d},
                device_id_type=pl.DeviceIdType.MESH,
            ).start()

        @pl.when(d == me)
        def _():
            pltpu.make_async_copy(gsend.at[row, d], g_out.at[me * ROWS + row], lsem.at[row]).start()

    def row_body(row, carry):
        def chunk_body(c, carry):
            n = row * CHUNKS + c
            slot = lax.rem(n, SLOTS)
            a_copy(n).wait()
            for u in range(CHUNK):
                t = jnp.dot(cot[...], abuf[slot, u], preferred_element_type=F32)
                base = pl.multiple_of((c * CHUNK + u) * PITCH, 8)
                ts0[pl.ds(base, PITCH), :] = t[:, 0:LANES]
                ts1[pl.ds(base, PITCH), 0 : AO - LANES] = t[:, LANES:AO]

            @pl.when(n + SLOTS < ROWS * CHUNKS)
            def _():
                a_copy(n + SLOTS).start()

            return carry

        lax.fori_loop(0, CHUNKS, chunk_body, 0)

        g = {}

        def half(j):
            lhs = jnp.concatenate(
                [ts0[pl.ds(j, AO, stride=PITCH), :], ts1[pl.ds(j, AO, stride=PITCH), :]], axis=1
            ).astype(BF16)
            return jnp.dot(lhs, cvp[...], preferred_element_type=F32).astype(BF16)

        def need(j):
            if j in g:
                return
            if j + 1 < OCC:
                h = jnp.concatenate([half(j), half(j + 1)], axis=1)
                both = jnp.dot(cvt[:, 0:AO], h, preferred_element_type=F32)
                g[j], g[j + 1] = both[:, 0:LANES], both[:, LANES : 2 * LANES]
            else:
                g[j] = jnp.dot(cvt[:, 0:AO], half(j), preferred_element_type=F32)

        for d in range(DEVS):
            first = PAIRS * d
            j0, j1 = first // VIRT, (first + PAIRS - 1) // VIRT
            rolled = {}
            for j in range(j0, j1 + 1):
                need(j)
                shift = (VIRT * j - first) % LANES
                rolled[j] = pltpu.roll(g[j], shift, axis=1) if shift else g[j]
            tiles = []
            for t in range(4):
                lo = first + LANES * t
                hi = min(lo + LANES, first + PAIRS)
                ja, jb = lo // VIRT, (hi - 1) // VIRT
                tile = rolled[ja]
                for j in range(ja + 1, jb + 1):
                    tile = jnp.where(lane >= VIRT * j - lo, rolled[j], tile)
                tiles.append(tile)
            last = tiles.pop()
            tiles.append(jnp.where(lane56 < 64, last[0:56], pltpu.roll(last[48:VIRT], 64, axis=1)))
            gsend[row, d] = jnp.concatenate(tiles, axis=0).astype(BF16)
            if d:
                send(row, d - 1)
        send(row, DEVS - 1)
        return carry

    lax.fori_loop(0, ROWS, row_body, 0)

    def drain(row, carry):
        for k in range(DEVS):
            @pl.when(k != me)
            def _():
                pltpu.make_async_remote_copy(
                    src_ref=gsend.at[row, k],
                    dst_ref=g_out.at[k * ROWS + row],
                    send_sem=ssem.at[row, k],
                    recv_sem=rsem.at[row, k],
                    device_id={"dev": k},
                    device_id_type=pl.DeviceIdType.MESH,
                ).wait()

        pltpu.make_async_copy(gsend.at[row, 0], g_out.at[me * ROWS + row], lsem.at[row]).wait()
        return carry

    lax.fori_loop(0, ROWS, drain, 0)


def _exchange(ao_rows, cot, cv):
    return pl.pallas_call(
        _exchange_kernel,
        out_shape=jax.ShapeDtypeStruct((AO, BLK, LANES), BF16),
        in_specs=[
            pl.BlockSpec(memory_space=pl.ANY),
            pl.BlockSpec(memory_space=pltpu.VMEM),
            pl.BlockSpec(memory_space=pltpu.VMEM),
        ],
        out_specs=pl.BlockSpec(memory_space=pl.ANY),
        scratch_shapes=[
            pltpu.VMEM((SLOTS, CHUNK, AO, AO), BF16),
            pltpu.VMEM((PITCH, AO), BF16),
            pltpu.VMEM((2 * LANES, LANES), BF16),
            pltpu.VMEM((VIRT, 2 * LANES), BF16),
            pltpu.VMEM((AO * PITCH, LANES), F32),
            pltpu.VMEM((AO * PITCH, LANES), F32),
            pltpu.VMEM((ROWS, DEVS, BLK, LANES), BF16),
            pltpu.SemaphoreType.DMA((SLOTS,)),
            pltpu.SemaphoreType.DMA((ROWS, DEVS)),
            pltpu.SemaphoreType.DMA((ROWS, DEVS)),
            pltpu.SemaphoreType.DMA((ROWS,)),
        ],
        compiler_params=pltpu.CompilerParams(
            collective_id=0, has_side_effects=True, vmem_limit_bytes=62 * 1024 * 1024
        ),
        name="exchange",
    )(ao_rows, cot, cv)


def _last_kernel(lhs_ref, g_ref, out_ref):
    step = pl.program_id(0)
    x = g_ref[...].astype(F32)
    low = x[:, 0:8, :].reshape(AO * 8, LANES)
    high = x[:, 8:16, :].reshape(AO * 8, LANES)
    rhs = jnp.concatenate([low, high], axis=1).astype(BF16)
    v = jnp.dot(lhs_ref[...], rhs, preferred_element_type=F32)
    for u in range(2):
        part = v[:, u * LANES : (u + 1) * LANES].reshape(OCC, 8, LANES)
        m = 2 * step + u

        @pl.when(m < 39)
        def _():
            rows = pl.ds(pl.multiple_of(lax.rem(m, 13) * 8, 8), 8)
            cols = pl.ds(pl.multiple_of(m // 13 * LANES, LANES), LANES)
            out_ref[:, rows, cols] = part

        @pl.when(m >= 39)
        def _():
            k = (m - 39) * 8
            out_ref[:, pl.ds(pl.multiple_of(k, 8), 8), 384:PAIRS] = part[:, :, 0 : PAIRS - 384]

        @pl.when(m >= 40)
        def _():
            k = (m - 39) * 8 + 48
            moved = pltpu.roll(part, 64, axis=2)
            out_ref[:, pl.ds(pl.multiple_of(k, 8), 8), 384:PAIRS] = moved[:, :, 0 : PAIRS - 384]


def _last(lhs, g):
    return pl.pallas_call(
        _last_kernel,
        grid=(BLK // 16,),
        out_shape=jax.ShapeDtypeStruct((OCC, VIRT, PAIRS), F32),
        in_specs=[
            pl.BlockSpec((OCC * 8, AO * 8), lambda s: (0, 0)),
            pl.BlockSpec((AO, 16, LANES), lambda s: (0, s, 0)),
        ],
        out_specs=pl.BlockSpec((OCC, VIRT, PAIRS), lambda s: (0, 0, 0)),
        compiler_params=pltpu.CompilerParams(vmem_limit_bytes=50 * 1024 * 1024),
        name="last",
    )(lhs, g)


def solution(mesh):
    def local_part(ao_rows, occ_coef, virt_coef):
        g = _exchange(ao_rows, occ_coef.T, virt_coef)
        lhs = jnp.kron(occ_coef.T, jnp.eye(8, dtype=BF16))
        return _last(lhs, g)

    return jax.shard_map(
        local_part,
        mesh=mesh,
        in_specs=(P(("frag", "dev"), None, None, None), P("frag", None), P("frag", None)),
        out_specs=P("frag", None, "dev"),
        check_vma=False,
    )
```

time: 670 us -> 210 us (0.31)
  local copies, waits for them, and re-layouts: 295 us -> 10.1 us
  blocking collectives: 225 us -> 0 us
  Pallas kernels: 0 us -> 194 us
  matrix products: 147 us -> 0 us
    all_to_all x1 -> x0, blocking collectives: 225 us -> none  [local_part(): pair_block = lax.all_to_all(half_ints, 'dev', 2, 0, tiled=True)]
    pallas_call x0 -> x2, Pallas kernels: none -> 194 us  [the longest x1 172 us: _exchange(): pl.pallas_call(_exchange_kernel, out_shape=jax.ShapeDtypeStruct((AO, BLK,...]
    unnamed x6 -> x0, local copies, waits for them, and re-layouts: 181 us -> none
    dot_general x4 -> x0, matrix products: 147 us -> none  [the longest x1 88 us: local_part(): jnp.einsum('pqrs,rj->pqsj', ao_rows, occ_coef, preferred_element_type=jnp...]
    all_to_all x1 -> x0, local copies, waits for them, and re-layouts: 55.5 us -> none  [local_part(): pair_block = lax.all_to_all(half_ints, 'dev', 2, 0, tiled=True)]
    reshape x1 -> x0, local copies, waits for them, and re-layouts: 51 us -> none  [local_part(): half_ints = half_ints.reshape(rows_here, ao_dim, occ_dim * virt_dim)]
    mul x0 -> x1, local copies, waits for them, and re-layouts: none -> 10.1 us  [local_part(): lhs = jnp.kron(occ_coef.T, jnp.eye(8, dtype=BF16))]
    dot_general x1 -> x0, local copies, waits for them, and re-layouts: 7.01 us -> none  [local_part(): jnp.einsum('pi,apc->iac', occ_coef, three_quarter, preferred_element_type...]
where the time goes in v1:
time: 210 us; the launch traced here: 209 us
  Pallas kernels  194 us (92%)
  local copies, waits for them, and re-layouts  10.1 us (5%)
  other arithmetic  5.38 us (3%)
    pallas_call x1, Pallas kernels, _exchange(): pl.pallas_call(_exchange_kernel, out_shape=jax.ShapeDtypeStruct((AO, BLK,...  172 us
    pallas_call x1, Pallas kernels, _last(): pl.pallas_call(_last_kernel, grid=(BLK // 16,), out_shape=jax.ShapeDtypeS...  21.8 us
    mul x1, local copies, waits for them, and re-layouts, local_part(): lhs = jnp.kron(occ_coef.T, jnp.eye(8, dtype=BF16))  10.1 us
    mul x1, other arithmetic, local_part(): lhs = jnp.kron(occ_coef.T, jnp.eye(8, dtype=BF16))  5.38 us

profile of v1, /device:TPU:0, one launch (start us, length us, event | category | flops | bytes accessed | tf_op | source)
XLA Modules:
  0.0 209.1 jit_solution(2753897343152764569)
XLA Ops:
  0.0 5.4 %broadcast_multiply_fusion = bf16[33,8,152,8]{3,2,1,0:T(8,128)(2,1)} fusion(bf16[8,8]{1,0:T(8,128)(2,1)S(1)} %fusion, bf16[33,152]{1,0:T(8,128)(2,1)} %bitcast.3), kind=kLoop, calls=%fused_computation | loop fusion | flops 321024 | bytes 652208 | tf_op jit(solution)/shard_map/jit(kron)/mul | solution.py:231
  5.4 10.1 %mul.27.lhs_ref = bf16[264,1216]{1,0:T(8,128)(2,1)S(1)} reshape(bf16[33,8,152,8]{3,2,1,0:T(8,128)(2,1)} %broadcast_multiply_fusion) | data formatting | bytes 1284096 | tf_op jit(solution)/shard_map/jit(kron)/mul | solution.py:231
  15.5 171.7 %exchange.1.g_ref = bf16[152,368,128]{2,1,0:T(8,128)(2,1)} custom-call(bf16[19,152,152,152]{3,2,1,0:T(8,128)(2,1)} %a_hbm.1, bf16[33,152]{1,0:T(8,128)(2,1)} %bitcast.4, bf16[152,104]{1,0:T(8,128)(2,1)} %cv_ref.1), custom_call_target="tpu_custom_call" | custom-call | tf_op jit(solution)/shard_map/exchange/pallas_call | solution.py:155
  187.3 21.8 %last.1 = f32[33,104,429]{2,1,0:T(8,128)} custom-call(bf16[264,1216]{1,0:T(8,128)(2,1)S(1)} %mul.27.lhs_ref, bf16[152,368,128]{2,1,0:T(8,128)(2,1)} %exchange.1.g_ref), custom_call_target="tpu_custom_call" | custom-call | tf_op jit(solution)/shard_map/last/pallas_call | solution.py:214
  (1 shorter events, 0.0 us)

commit v2 on v1

v2 whole, which is shorter than its diff:
```python
import functools

import jax
import jax.numpy as jnp
from jax import lax
from jax.experimental import pallas as pl
from jax.experimental.pallas import tpu as pltpu
from jax.sharding import PartitionSpec as P

F32 = jnp.float32
BF16 = jnp.bfloat16
AO, OCC, VIRT = 152, 33, 104
DEVS = 8
ROWS = AO // DEVS
PAIRS = OCC * VIRT // DEVS
PITCH = 40
CHUNK = 19
CHUNKS = AO // CHUNK
SLOTS = 6
LANES = 128
TILES = VIRT // 8
REST = PAIRS - 3 * LANES
RTILES = -(-TILES * REST // LANES)
BLK = 8 * (3 * TILES + RTILES)
EARLY = 16
LATE = ROWS - EARLY


def _step4(lhs_ref, load, put, rest, lane8):
    depth = lhs_ref.shape[1]

    def group(g):
        return load(g).reshape(depth, LANES)

    def product(groups):
        rhs = jnp.concatenate([group(g) for g in groups], axis=1)
        return jnp.dot(lhs_ref[...], rhs, preferred_element_type=F32).reshape(OCC, 16, len(groups) * LANES)

    def tile(v, m):
        g, u = divmod(m, 2)
        return v[:, 8 * u : 8 * u + 8, g * LANES : (g + 1) * LANES]

    base = 18
    v = product([base + k for k in range(BLK // 16 - base)])
    tail = [tile(v, k) for k in range(3)]
    packed = [tile(v, 3 + k) for k in range(RTILES)]
    for n in range(TILES):
        start = REST * n
        k0, k1 = start // LANES, (start + REST - 1) // LANES
        back = (-start) % LANES
        piece = pltpu.roll(packed[k0], back, axis=2) if back else packed[k0]
        if k1 != k0:
            other = pltpu.roll(packed[k1], back, axis=2)
            piece = jnp.where(lane8 < LANES * k1 - start, piece, other)
        rest[:, 8 * n : 8 * n + 8, :] = piece

    def pair(e, carry):
        v = product([3 * e, 3 * e + 1, 3 * e + 2])
        put(e, 2, [tile(v, m) for m in range(6)])
        return carry

    lax.fori_loop(0, TILES // 2, pair, 0)
    put(TILES // 2, 1, tail)


def _spread(cot_f32, width, owner):
    k = lax.broadcasted_iota(jnp.int32, (AO, width), 1)
    p = lax.broadcasted_iota(jnp.int32, (AO, width), 0)
    pick = jnp.where(p == owner(k // 16), 1.0, 0.0).astype(BF16)
    wide = jnp.dot(cot_f32, pick, preferred_element_type=F32)[0:OCC]
    a = lax.broadcasted_iota(jnp.int32, (16, width), 0)
    ka = lax.rem(lax.broadcasted_iota(jnp.int32, (16, width), 1), 16)
    keep = (a == ka)[None]
    return jnp.where(keep, wide[:, None, :], 0.0).reshape(OCC * 16, width).astype(BF16)


def _exchange_kernel(
    a_hbm, cot_ref, cv_ref, v_out, g_out, lhs_out,
    abuf, cot, cvp, cvt, ts0, ts1, gsend, grecv, vacc, rest, lhs, late,
    asem, ssem, rsem, lsem, vsem, hsem,
):
    me = lax.axis_index("dev")

    def a_copy(n):
        return pltpu.make_async_copy(
            a_hbm.at[n // CHUNKS, pl.ds(lax.rem(n, CHUNKS) * CHUNK, CHUNK)],
            abuf.at[lax.rem(n, SLOTS)],
            asem.at[lax.rem(n, SLOTS)],
        )

    for n in range(SLOTS):
        a_copy(n).start()

    barrier = pltpu.get_barrier_semaphore()
    for k in range(1, DEVS):
        pl.semaphore_signal(
            barrier, inc=1, device_id={"dev": lax.rem(me + k, DEVS)}, device_id_type=pl.DeviceIdType.MESH
        )

    cot[...] = jnp.zeros_like(cot)
    cot[0:OCC, :] = cot_ref[...]
    cvp[...] = jnp.zeros_like(cvp)
    cvp[0:AO, 0:VIRT] = cv_ref[...]
    cvt[...] = cvp[...].astype(F32).T[0:VIRT, :].astype(BF16)
    ts1[...] = jnp.zeros_like(ts1)

    pl.semaphore_wait(barrier, DEVS - 1)

    lane = lax.broadcasted_iota(jnp.int32, (VIRT, LANES), 1)
    lane8 = lax.broadcasted_iota(jnp.int32, (8, LANES), 1)

    def early_copy(row, src, dst):
        return pltpu.make_async_remote_copy(
            src_ref=gsend.at[row, dst],
            dst_ref=grecv.at[src * EARLY + row],
            send_sem=ssem.at[row, dst],
            recv_sem=rsem.at[row, src],
            device_id={"dev": dst},
            device_id_type=pl.DeviceIdType.MESH,
        )

    def late_copy(row, src, dst):
        return pltpu.make_async_remote_copy(
            src_ref=gsend.at[row, dst],
            dst_ref=g_out.at[src * LATE + row - EARLY],
            send_sem=ssem.at[row, dst],
            recv_sem=rsem.at[row, src],
            device_id={"dev": dst},
            device_id_type=pl.DeviceIdType.MESH,
        )

    def own_copy(row):
        return pltpu.make_async_copy(gsend.at[row, me], g_out.at[me * LATE + row - EARLY], lsem.at[row - EARLY])

    def send(row, d):
        @pl.when((d != me) & (row < EARLY))
        def _():
            early_copy(row, me, d).start()

        @pl.when((d != me) & (row >= EARLY))
        def _():
            late_copy(row, me, d).start()

        @pl.when((d == me) & (row < EARLY))
        def _():
            grecv[me * EARLY + row] = gsend[row, d]

        @pl.when((d == me) & (row >= EARLY))
        def _():
            own_copy(row).start()

    def row_body(row, carry):
        def chunk_body(c, carry):
            n = row * CHUNKS + c
            slot = lax.rem(n, SLOTS)
            a_copy(n).wait()
            for u in range(CHUNK):
                t = jnp.dot(cot[...], abuf[slot, u], preferred_element_type=F32)
                base = pl.multiple_of((c * CHUNK + u) * PITCH, 8)
                ts0[pl.ds(base, PITCH), :] = t[:, 0:LANES]
                ts1[pl.ds(base, PITCH), 0 : AO - LANES] = t[:, LANES:AO]

            @pl.when(n + SLOTS < ROWS * CHUNKS)
            def _():
                a_copy(n + SLOTS).start()

            return carry

        lax.fori_loop(0, CHUNKS, chunk_body, 0)

        g = {}

        def half(j):
            lhs = jnp.concatenate(
                [ts0[pl.ds(j, AO, stride=PITCH), :], ts1[pl.ds(j, AO, stride=PITCH), :]], axis=1
            ).astype(BF16)
            return jnp.dot(lhs, cvp[...], preferred_element_type=F32).astype(BF16)

        def need(j):
            if j in g:
                return
            if j + 1 < OCC:
                h = jnp.concatenate([half(j), half(j + 1)], axis=1)
                both = jnp.dot(cvt[:, 0:AO], h, preferred_element_type=F32)
                g[j], g[j + 1] = both[:, 0:LANES], both[:, LANES : 2 * LANES]
            else:
                g[j] = jnp.dot(cvt[:, 0:AO], half(j), preferred_element_type=F32)

        for d in range(DEVS):
            first = PAIRS * d
            j0, j1 = first // VIRT, (first + PAIRS - 1) // VIRT
            rolled = {}
            for j in range(j0, j1 + 1):
                need(j)
                shift = (VIRT * j - first) % LANES
                rolled[j] = pltpu.roll(g[j], shift, axis=1) if shift else g[j]
            tiles = []
            for t in range(4):
                lo = first + LANES * t
                hi = min(lo + LANES, first + PAIRS)
                ja, jb = lo // VIRT, (hi - 1) // VIRT
                tile = rolled[ja]
                for j in range(ja + 1, jb + 1):
                    tile = jnp.where(lane >= VIRT * j - lo, rolled[j], tile)
                tiles.append(tile)
            last = tiles.pop()
            parts = [tile[8 * n : 8 * n + 8] for n in range(TILES) for tile in tiles]
            moved = []
            for n in range(TILES):
                shift = REST * n % LANES
                piece = last[8 * n : 8 * n + 8]
                moved.append(pltpu.roll(piece, shift, axis=1) if shift else piece)
            for k in range(RTILES):
                n0, n1 = LANES * k // REST, min((LANES * k + LANES - 1) // REST, TILES - 1)
                part = moved[n0]
                for n in range(n0 + 1, n1 + 1):
                    part = jnp.where(lane8 >= REST * n - LANES * k, moved[n], part)
                parts.append(part)
            gsend[row, d] = jnp.concatenate(parts, axis=0).astype(BF16)
            if d:
                send(row, d - 1)
        send(row, DEVS - 1)
        return carry

    lax.fori_loop(0, ROWS, row_body, 0)

    vacc[...] = jnp.zeros_like(vacc)
    for s in range(DEVS):
        cols = slice(s * EARLY * 16, (s + 1) * EARLY * 16)
        lhs[:, cols] = _spread(cot[...], EARLY * 16, lambda q: s * ROWS + q)
    late[...] = _spread(cot[...], DEVS * LATE * 16, lambda q: q // LATE * ROWS + EARLY + lax.rem(q, LATE))
    late_out = pltpu.make_async_copy(late, lhs_out, hsem)
    late_out.start()

    def arrived(row, carry):
        for k in range(DEVS):
            @pl.when(k != me)
            def _():
                early_copy(row, k, me).wait_recv()

        return carry

    lax.fori_loop(0, EARLY, arrived, 0)

    def v_copy(e, width):
        rows = pl.ds(pl.multiple_of(e * 16, 8), 8 * width)
        return pltpu.make_async_copy(vacc.at[:, rows, :], v_out.at[:, rows, :], vsem.at[e])

    def put(e, width, tiles):
        for w in range(width):
            rows = pl.ds(pl.multiple_of(e * 16 + 8 * w, 8), 8)
            for t in range(3):
                vacc[:, rows, t * LANES : (t + 1) * LANES] += tiles[3 * w + t]
            vacc[:, rows, 3 * LANES : PAIRS] = rest[:, rows, 0:REST]
        v_copy(e, width).start()

    def load(g):
        return grecv[:, pl.ds(pl.multiple_of(g * 16, 16), 16), :]

    _step4(lhs, load, put, rest, lane8)

    def arrived_late(row, carry):
        for k in range(DEVS):
            @pl.when(k != me)
            def _():
                late_copy(row, k, me).wait_recv()

        own_copy(row).wait()
        return carry

    lax.fori_loop(EARLY, ROWS, arrived_late, 0)

    def sent(row, carry):
        for k in range(DEVS):
            @pl.when(k != me)
            def _():
                pltpu.make_async_remote_copy(
                    src_ref=gsend.at[row, k],
                    dst_ref=g_out.at[0],
                    send_sem=ssem.at[row, k],
                    recv_sem=rsem.at[row, k],
                    device_id={"dev": k},
                    device_id_type=pl.DeviceIdType.MESH,
                ).wait_send()

        return carry

    lax.fori_loop(0, ROWS, sent, 0)

    def stored(e, carry):
        v_copy(e, 2).wait()
        return carry

    lax.fori_loop(0, TILES // 2, stored, 0)
    v_copy(TILES // 2, 1).wait()
    late_out.wait()


def _exchange(ao_rows, cot, cv):
    return pl.pallas_call(
        _exchange_kernel,
        out_shape=(
            jax.ShapeDtypeStruct((OCC, VIRT, PAIRS), F32),
            jax.ShapeDtypeStruct((DEVS * LATE, BLK, LANES), BF16),
            jax.ShapeDtypeStruct((OCC * 16, DEVS * LATE * 16), BF16),
        ),
        in_specs=[
            pl.BlockSpec(memory_space=pl.ANY),
            pl.BlockSpec(memory_space=pltpu.VMEM),
            pl.BlockSpec(memory_space=pltpu.VMEM),
        ],
        out_specs=tuple(pl.BlockSpec(memory_space=pl.ANY) for _ in range(3)),
        scratch_shapes=[
            pltpu.VMEM((SLOTS, CHUNK, AO, AO), BF16),
            pltpu.VMEM((PITCH, AO), BF16),
            pltpu.VMEM((2 * LANES, LANES), BF16),
            pltpu.VMEM((VIRT, 2 * LANES), BF16),
            pltpu.VMEM((AO * PITCH, LANES), F32),
            pltpu.VMEM((AO * PITCH, LANES), F32),
            pltpu.VMEM((ROWS, DEVS, BLK, LANES), BF16),
            pltpu.VMEM((DEVS * EARLY, BLK, LANES), BF16),
            pltpu.VMEM((OCC, VIRT, PAIRS), F32),
            pltpu.VMEM((OCC, VIRT, LANES), F32),
            pltpu.VMEM((OCC * 16, DEVS * EARLY * 16), BF16),
            pltpu.VMEM((OCC * 16, DEVS * LATE * 16), BF16),
            pltpu.SemaphoreType.DMA((SLOTS,)),
            pltpu.SemaphoreType.DMA((ROWS, DEVS)),
            pltpu.SemaphoreType.DMA((ROWS, DEVS)),
            pltpu.SemaphoreType.DMA((LATE,)),
            pltpu.SemaphoreType.DMA((TILES // 2 + 1,)),
            pltpu.SemaphoreType.DMA,
        ],
        compiler_params=pltpu.CompilerParams(
            collective_id=0, has_side_effects=True, vmem_limit_bytes=63 * 1024 * 1024
        ),
        name="exchange",
    )(ao_rows, cot, cv)


def _last_kernel(lhs_ref, g_ref, v_hbm, out_hbm, vbuf, rest, isem, osem):
    lane8 = lax.broadcasted_iota(jnp.int32, (8, LANES), 1)

    def part(e, width, ref, into, sem):
        rows = pl.ds(pl.multiple_of(e * 16, 8), 8 * width)
        src, dst = ref.at[:, rows, :], vbuf.at[:, rows, :]
        return pltpu.make_async_copy(src, dst, sem.at[e]) if into else pltpu.make_async_copy(dst, src, sem.at[e])

    for e in range(TILES // 2):
        part(e, 2, v_hbm, True, isem).start()
    part(TILES // 2, 1, v_hbm, True, isem).start()

    def put(e, width, tiles):
        part(e, width, v_hbm, True, isem).wait()
        for w in range(width):
            rows = pl.ds(pl.multiple_of(e * 16 + 8 * w, 8), 8)
            for t in range(3):
                vbuf[:, rows, t * LANES : (t + 1) * LANES] += tiles[3 * w + t]
            vbuf[:, rows, 3 * LANES : PAIRS] += rest[:, rows, 0:REST]
        part(e, width, out_hbm, False, osem).start()

    def load(g):
        return g_ref[:, pl.ds(pl.multiple_of(g * 16, 16), 16), :]

    _step4(lhs_ref, load, put, rest, lane8)

    for e in range(TILES // 2):
        part(e, 2, out_hbm, False, osem).wait()
    part(TILES // 2, 1, out_hbm, False, osem).wait()


def _last(lhs, g, v):
    return pl.pallas_call(
        _last_kernel,
        out_shape=jax.ShapeDtypeStruct((OCC, VIRT, PAIRS), F32),
        in_specs=[
            pl.BlockSpec(memory_space=pltpu.VMEM),
            pl.BlockSpec(memory_space=pltpu.VMEM),
            pl.BlockSpec(memory_space=pl.ANY),
        ],
        out_specs=pl.BlockSpec(memory_space=pl.ANY),
        scratch_shapes=[
            pltpu.VMEM((OCC, VIRT, PAIRS), F32),
            pltpu.VMEM((OCC, VIRT, LANES), F32),
            pltpu.SemaphoreType.DMA((TILES // 2 + 1,)),
            pltpu.SemaphoreType.DMA((TILES // 2 + 1,)),
        ],
        compiler_params=pltpu.CompilerParams(vmem_limit_bytes=50 * 1024 * 1024),
        name="last",
    )(lhs, g, v)


def solution(mesh):
    def local_part(ao_rows, occ_coef, virt_coef):
        v, g, lhs = _exchange(ao_rows, occ_coef.T, virt_coef)
        return _last(lhs, g, v)

    return jax.shard_map(
        local_part,
        mesh=mesh,
        in_specs=(P(("frag", "dev"), None, None, None), P("frag", None), P("frag", None)),
        out_specs=P("frag", None, "dev"),
        check_vma=False,
    )
```

time: 210 us -> 187 us (0.89)
  Pallas kernels: 194 us -> 184 us
  local copies, waits for them, and re-layouts: 10.1 us -> 2.6 us
  other arithmetic: 5.38 us -> 0 us
    mul x1 -> x0, local copies, waits for them, and re-layouts: 10.1 us -> none  [local_part(): lhs = jnp.kron(occ_coef.T, jnp.eye(8, dtype=BF16))]
    pallas_call x2, Pallas kernels: 194 us -> 184 us  [the longest x1 178 us: _exchange(): pl.pallas_call(_exchange_kernel, out_shape=(jax.ShapeDtypeStruct((OCC, VI...]
    mul x1 -> x0, other arithmetic: 5.38 us -> none  [local_part(): lhs = jnp.kron(occ_coef.T, jnp.eye(8, dtype=BF16))]
    unnamed x0 -> x4, local copies, waits for them, and re-layouts: none -> 2.6 us
where the time goes in v2:
time: 187 us
  Pallas kernels  184 us (98%)
  local copies, waits for them, and re-layouts  2.6 us (1%)
    pallas_call x1, Pallas kernels, _exchange(): pl.pallas_call(_exchange_kernel, out_shape=(jax.ShapeDtypeStruct((OCC, VI...  178 us
    pallas_call x1, Pallas kernels, _last(): pl.pallas_call(_last_kernel, out_shape=jax.ShapeDtypeStruct((OCC, VIRT, P...  6.41 us

profile of v2, /device:TPU:0, one launch (start us, length us, event | category | flops | bytes accessed | tf_op | source)
XLA Modules:
  0.0 186.8 jit_solution(12162733844238619995)
XLA Ops:
  0.0 177.8 %exchange.1 = (f32[33,104,429]{2,1,0:T(8,128)}, bf16[24,352,128]{2,1,0:T(8,128)(2,1)}, bf16[528,384]{1,0:T(8,128)(2,1)}) custom-call(bf16[19,152,152,152]{3,2,1,0:T(8,128)(2,1)} %a_hbm.1, bf16[33,152]{1,0:T(8,128)(2,1)} %bitcast.1, bf16[152,104]{1,0:T(8,128)(2,1)} %cv_ref.1), custom_call_target="tpu_custom_call" | custom-call | tf_op jit(solution)/shard_map/exchange/pallas_call | solution.py:300
  177.8 0.0 copy-start
  177.8 1.6 copy-done
  179.4 0.0 copy-start.1
  179.4 1.0 copy-done.1
  180.4 6.4 %last.1 = f32[33,104,429]{2,1,0:T(8,128)} custom-call(bf16[528,384]{1,0:T(8,128)(2,1)S(1)} %copy-done.1, bf16[24,352,128]{2,1,0:T(8,128)(2,1)S(1)} %copy-done, f32[33,104,429]{2,1,0:T(8,128)} %get-tuple-element.10.v_hbm), custom_call_target="tpu_custom_call" | custom-call | tf_op jit(solution)/shard_map/last/pallas_call | solution.py:372
Async XLA Ops:
  177.8 1.6 copy-start
  179.4 1.0 copy-start.1

commit v3 on v2

--- a/solution.py
+++ b/solution.py
@@ -22,6 +22,7 @@
 REST = PAIRS - 3 * LANES
 RTILES = -(-TILES * REST // LANES)
 BLK = 8 * (3 * TILES + RTILES)
+GROUPS = ((0, 1, 2, 3, 4, 5), (6, 7, 8, 9, 10, 11, 12, 13), (14, 15, 16, 17, 18, 19, 20, 21), (22, 23, 24, 25, 26, 27, 28, 29, 30, 31, 32))
 EARLY = 16
 LATE = ROWS - EARLY
 
@@ -100,9 +101,9 @@
     cot[...] = jnp.zeros_like(cot)
     cot[0:OCC, :] = cot_ref[...]
     cvp[...] = jnp.zeros_like(cvp)
-    cvp[0:AO, 0:VIRT] = cv_ref[...]
-    cvt[...] = cvp[...].astype(F32).T[0:VIRT, :].astype(BF16)
-    ts1[...] = jnp.zeros_like(ts1)
+    cvp[:, 0:VIRT] = cv_ref[...]
+    square = jnp.concatenate([cvp[...].astype(F32), jnp.zeros((2 * LANES - AO, LANES), F32)], axis=0)
+    cvt[...] = square.T[0:VIRT, 0:AO].astype(BF16)
 
     pl.semaphore_wait(barrier, DEVS - 1)
 
@@ -170,21 +171,23 @@
 
         g = {}
 
-        def half(j):
-            lhs = jnp.concatenate(
-                [ts0[pl.ds(j, AO, stride=PITCH), :], ts1[pl.ds(j, AO, stride=PITCH), :]], axis=1
-            ).astype(BF16)
-            return jnp.dot(lhs, cvp[...], preferred_element_type=F32).astype(BF16)
-
         def need(j):
             if j in g:
                 return
-            if j + 1 < OCC:
-                h = jnp.concatenate([half(j), half(j + 1)], axis=1)
-                both = jnp.dot(cvt[:, 0:AO], h, preferred_element_type=F32)
-                g[j], g[j + 1] = both[:, 0:LANES], both[:, LANES : 2 * LANES]
-            else:
-                g[j] = jnp.dot(cvt[:, 0:AO], half(j), preferred_element_type=F32)
+            group = next(js for js in GROUPS if j in js)
+            lhs = jnp.concatenate(
+                [
+                    jnp.concatenate([(ts0, ts1)[k][pl.ds(jj, AO, stride=PITCH), :] for jj in group], axis=0)
+                    for k in range(2)
+                ],
+                axis=1,
+            )
+            lhs = lhs[:, 0:AO].astype(BF16)
+            half = jnp.dot(lhs, cvp[...], preferred_element_type=F32)
+            wide = jnp.concatenate([half[AO * n : AO * n + AO] for n in range(len(group))], axis=1).astype(BF16)
+            full = jnp.dot(cvt[...], wide, preferred_element_type=F32)
+            for n, jj in enumerate(group):
+                g[jj] = full[:, LANES * n : LANES * n + LANES]
 
         for d in range(DEVS):
             first = PAIRS * d
@@ -313,8 +316,8 @@
         scratch_shapes=[
             pltpu.VMEM((SLOTS, CHUNK, AO, AO), BF16),
             pltpu.VMEM((PITCH, AO), BF16),
-            pltpu.VMEM((2 * LANES, LANES), BF16),
-            pltpu.VMEM((VIRT, 2 * LANES), BF16),
+            pltpu.VMEM((AO, LANES), BF16),
+            pltpu.VMEM((VIRT, AO), BF16),
             pltpu.VMEM((AO * PITCH, LANES), F32),
             pltpu.VMEM((AO * PITCH, LANES), F32),
             pltpu.VMEM((ROWS, DEVS, BLK, LANES), BF16),

time: 187 us -> 170 us (0.909)
  Pallas kernels: 184 us -> 167 us
    pallas_call x1, Pallas kernels: 178 us -> 161 us  [_exchange(): pl.pallas_call(_exchange_kernel, out_shape=(jax.ShapeDtypeStruct((OCC, VI...]
where the time goes in v3:
time: 170 us
  Pallas kernels  167 us (98%)
  local copies, waits for them, and re-layouts  2.6 us (2%)
    pallas_call x1, Pallas kernels, _exchange(): pl.pallas_call(_exchange_kernel, out_shape=(jax.ShapeDtypeStruct((OCC, VI...  161 us
    pallas_call x1, Pallas kernels, _last(): pl.pallas_call(_last_kernel, out_shape=jax.ShapeDtypeStruct((OCC, VIRT, P...  6.41 us

profile of v3, /device:TPU:0, one launch (start us, length us, event | category | flops | bytes accessed | tf_op | source)
XLA Modules:
  0.0 170.1 jit_solution(12532273734710296522)
XLA Ops:
  0.0 161.1 %exchange.1 = (f32[33,104,429]{2,1,0:T(8,128)}, bf16[24,352,128]{2,1,0:T(8,128)(2,1)}, bf16[528,384]{1,0:T(8,128)(2,1)}) custom-call(bf16[19,152,152,152]{3,2,1,0:T(8,128)(2,1)} %a_hbm.1, bf16[33,152]{1,0:T(8,128)(2,1)} %bitcast.1, bf16[152,104]{1,0:T(8,128)(2,1)} %cv_ref.1), custom_call_target="tpu_custom_call" | custom-call | tf_op jit(solution)/shard_map/exchange/pallas_call | solution.py:303
  161.1 0.0 copy-start
  161.1 1.6 copy-done
  162.7 0.0 copy-start.1
  162.7 1.0 copy-done.1
  163.7 6.4 %last.1 = f32[33,104,429]{2,1,0:T(8,128)} custom-call(bf16[528,384]{1,0:T(8,128)(2,1)S(1)} %copy-done.1, bf16[24,352,128]{2,1,0:T(8,128)(2,1)S(1)} %copy-done, f32[33,104,429]{2,1,0:T(8,128)} %get-tuple-element.10.v_hbm), custom_call_target="tpu_custom_call" | custom-call | tf_op jit(solution)/shard_map/last/pallas_call | solution.py:375
Async XLA Ops:
  161.1 1.6 copy-start
  162.7 1.0 copy-start.1

commit v4 on v3

--- a/solution.py
+++ b/solution.py
@@ -16,18 +16,19 @@
 PITCH = 40
 CHUNK = 19
 CHUNKS = AO // CHUNK
-SLOTS = 6
+SLOTS = 4
+RING = 10
 LANES = 128
 TILES = VIRT // 8
 REST = PAIRS - 3 * LANES
 RTILES = -(-TILES * REST // LANES)
 BLK = 8 * (3 * TILES + RTILES)
 GROUPS = ((0, 1, 2, 3, 4, 5), (6, 7, 8, 9, 10, 11, 12, 13), (14, 15, 16, 17, 18, 19, 20, 21), (22, 23, 24, 25, 26, 27, 28, 29, 30, 31, 32))
-EARLY = 16
+EARLY = 17
 LATE = ROWS - EARLY
 
 
-def _step4(lhs_ref, load, put, rest, lane8):
+def _step4(lhs_ref, load, put, rest, lane8, unroll):
     depth = lhs_ref.shape[1]
 
     def group(g):
@@ -60,7 +61,11 @@
         put(e, 2, [tile(v, m) for m in range(6)])
         return carry
 
-    lax.fori_loop(0, TILES // 2, pair, 0)
+    if unroll:
+        for e in range(TILES // 2):
+            pair(e, 0)
+    else:
+        lax.fori_loop(0, TILES // 2, pair, 0)
     put(TILES // 2, 1, tail)
 
 
@@ -77,8 +82,8 @@
 
 def _exchange_kernel(
     a_hbm, cot_ref, cv_ref, v_out, g_out, lhs_out,
-    abuf, cot, cvp, cvt, ts0, ts1, gsend, grecv, vacc, rest, lhs, late,
-    asem, ssem, rsem, lsem, vsem, hsem,
+    abuf, cot, cvp, cvt, ts0, ts1, gsend, grecv, rest, lhs,
+    asem, ssem, rsem,
 ):
     me = lax.axis_index("dev")
 
@@ -105,14 +110,12 @@
     square = jnp.concatenate([cvp[...].astype(F32), jnp.zeros((2 * LANES - AO, LANES), F32)], axis=0)
     cvt[...] = square.T[0:VIRT, 0:AO].astype(BF16)
 
-    pl.semaphore_wait(barrier, DEVS - 1)
-
     lane = lax.broadcasted_iota(jnp.int32, (VIRT, LANES), 1)
     lane8 = lax.broadcasted_iota(jnp.int32, (8, LANES), 1)
 
     def early_copy(row, src, dst):
         return pltpu.make_async_remote_copy(
-            src_ref=gsend.at[row, dst],
+            src_ref=gsend.at[lax.rem(row, RING), dst],
             dst_ref=grecv.at[src * EARLY + row],
             send_sem=ssem.at[row, dst],
             recv_sem=rsem.at[row, src],
@@ -120,19 +123,17 @@
             device_id_type=pl.DeviceIdType.MESH,
         )
 
-    def late_copy(row, src, dst):
+    def late_copy(row, src, dst, sems=None):
+        sems = row if sems is None else sems
         return pltpu.make_async_remote_copy(
-            src_ref=gsend.at[row, dst],
+            src_ref=gsend.at[lax.rem(row, RING), dst],
             dst_ref=g_out.at[src * LATE + row - EARLY],
-            send_sem=ssem.at[row, dst],
-            recv_sem=rsem.at[row, src],
+            send_sem=ssem.at[sems, dst],
+            recv_sem=rsem.at[sems, src],
             device_id={"dev": dst},
             device_id_type=pl.DeviceIdType.MESH,
         )
 
-    def own_copy(row):
-        return pltpu.make_async_copy(gsend.at[row, me], g_out.at[me * LATE + row - EARLY], lsem.at[row - EARLY])
-
     def send(row, d):
         @pl.when((d != me) & (row < EARLY))
         def _():
@@ -144,11 +145,17 @@
 
         @pl.when((d == me) & (row < EARLY))
         def _():
-            grecv[me * EARLY + row] = gsend[row, d]
+            grecv[me * EARLY + row] = gsend[lax.rem(row, RING), d]
 
         @pl.when((d == me) & (row >= EARLY))
         def _():
-            own_copy(row).start()
+            g_out[me * LATE + row - EARLY] = gsend[lax.rem(row, RING), d]
+
+    def sent(row):
+        for k in range(DEVS):
+            @pl.when(k != me)
+            def _():
+                late_copy(EARLY, me, k, row).wait_send()
 
     def row_body(row, carry):
         def chunk_body(c, carry):
@@ -168,6 +175,15 @@
             return carry
 
         lax.fori_loop(0, CHUNKS, chunk_body, 0)
+
+        @pl.when(row == 0)
+        def _():
+            pl.semaphore_wait(barrier, DEVS - 1)
+
+        @pl.when(row >= RING)
+        def _():
+            sent(row - RING)
+
 
         g = {}
 
@@ -219,7 +235,7 @@
                 for n in range(n0 + 1, n1 + 1):
                     part = jnp.where(lane8 >= REST * n - LANES * k, moved[n], part)
                 parts.append(part)
-            gsend[row, d] = jnp.concatenate(parts, axis=0).astype(BF16)
+            gsend[lax.rem(row, RING), d] = jnp.concatenate(parts, axis=0).astype(BF16)
             if d:
                 send(row, d - 1)
         send(row, DEVS - 1)
@@ -227,13 +243,11 @@
 
     lax.fori_loop(0, ROWS, row_body, 0)
 
-    vacc[...] = jnp.zeros_like(vacc)
+    v_out[...] = jnp.zeros_like(v_out)
     for s in range(DEVS):
         cols = slice(s * EARLY * 16, (s + 1) * EARLY * 16)
         lhs[:, cols] = _spread(cot[...], EARLY * 16, lambda q: s * ROWS + q)
-    late[...] = _spread(cot[...], DEVS * LATE * 16, lambda q: q // LATE * ROWS + EARLY + lax.rem(q, LATE))
-    late_out = pltpu.make_async_copy(late, lhs_out, hsem)
-    late_out.start()
+    lhs_out[...] = _spread(cot[...], DEVS * LATE * 16, lambda q: q // LATE * ROWS + EARLY + lax.rem(q, LATE))
 
     def arrived(row, carry):
         for k in range(DEVS):
@@ -245,22 +259,17 @@
 
     lax.fori_loop(0, EARLY, arrived, 0)
 
-    def v_copy(e, width):
-        rows = pl.ds(pl.multiple_of(e * 16, 8), 8 * width)
-        return pltpu.make_async_copy(vacc.at[:, rows, :], v_out.at[:, rows, :], vsem.at[e])
-
     def put(e, width, tiles):
         for w in range(width):
             rows = pl.ds(pl.multiple_of(e * 16 + 8 * w, 8), 8)
             for t in range(3):
-                vacc[:, rows, t * LANES : (t + 1) * LANES] += tiles[3 * w + t]
-            vacc[:, rows, 3 * LANES : PAIRS] = rest[:, rows, 0:REST]
-        v_copy(e, width).start()
+                v_out[:, rows, t * LANES : (t + 1) * LANES] += tiles[3 * w + t]
+            v_out[:, rows, 3 * LANES : PAIRS] = rest[:, rows, 0:REST]
 
     def load(g):
         return grecv[:, pl.ds(pl.multiple_of(g * 16, 16), 16), :]
 
-    _step4(lhs, load, put, rest, lane8)
+    _step4(lhs, load, put, rest, lane8, False)
 
     def arrived_late(row, carry):
         for k in range(DEVS):
@@ -268,35 +277,11 @@
             def _():
                 late_copy(row, k, me).wait_recv()
 
-        own_copy(row).wait()
         return carry
 
     lax.fori_loop(EARLY, ROWS, arrived_late, 0)
 
-    def sent(row, carry):
-        for k in range(DEVS):
-            @pl.when(k != me)
-            def _():
-                pltpu.make_async_remote_copy(
-                    src_ref=gsend.at[row, k],
-                    dst_ref=g_out.at[0],
-                    send_sem=ssem.at[row, k],
-                    recv_sem=rsem.at[row, k],
-                    device_id={"dev": k},
-                    device_id_type=pl.DeviceIdType.MESH,
-                ).wait_send()
-
-        return carry
-
-    lax.fori_loop(0, ROWS, sent, 0)
-
-    def stored(e, carry):
-        v_copy(e, 2).wait()
-        return carry
-
-    lax.fori_loop(0, TILES // 2, stored, 0)
-    v_copy(TILES // 2, 1).wait()
-    late_out.wait()
+    lax.fori_loop(ROWS - RING, ROWS, lambda row, carry: sent(row) or carry, 0)
 
 
 def _exchange(ao_rows, cot, cv):
@@ -307,12 +292,8 @@
             jax.ShapeDtypeStruct((DEVS * LATE, BLK, LANES), BF16),
             jax.ShapeDtypeStruct((OCC * 16, DEVS * LATE * 16), BF16),
         ),
-        in_specs=[
-            pl.BlockSpec(memory_space=pl.ANY),
-            pl.BlockSpec(memory_space=pltpu.VMEM),
-            pl.BlockSpec(memory_space=pltpu.VMEM),
-        ],
-        out_specs=tuple(pl.BlockSpec(memory_space=pl.ANY) for _ in range(3)),
+        in_specs=[pl.BlockSpec(memory_space=pl.ANY)] + [pl.BlockSpec(memory_space=pltpu.VMEM)] * 2,
+        out_specs=tuple(pl.BlockSpec(memory_space=pltpu.VMEM) for _ in range(3)),
         scratch_shapes=[
             pltpu.VMEM((SLOTS, CHUNK, AO, AO), BF16),
             pltpu.VMEM((PITCH, AO), BF16),
@@ -320,55 +301,44 @@
             pltpu.VMEM((VIRT, AO), BF16),
             pltpu.VMEM((AO * PITCH, LANES), F32),
             pltpu.VMEM((AO * PITCH, LANES), F32),
-            pltpu.VMEM((ROWS, DEVS, BLK, LANES), BF16),
+            pltpu.VMEM((RING, DEVS, BLK, LANES), BF16),
             pltpu.VMEM((DEVS * EARLY, BLK, LANES), BF16),
-            pltpu.VMEM((OCC, VIRT, PAIRS), F32),
             pltpu.VMEM((OCC, VIRT, LANES), F32),
             pltpu.VMEM((OCC * 16, DEVS * EARLY * 16), BF16),
-            pltpu.VMEM((OCC * 16, DEVS * LATE * 16), BF16),
             pltpu.SemaphoreType.DMA((SLOTS,)),
             pltpu.SemaphoreType.DMA((ROWS, DEVS)),
             pltpu.SemaphoreType.DMA((ROWS, DEVS)),
-            pltpu.SemaphoreType.DMA((LATE,)),
-            pltpu.SemaphoreType.DMA((TILES // 2 + 1,)),
-            pltpu.SemaphoreType.DMA,
         ],
         compiler_params=pltpu.CompilerParams(
-            collective_id=0, has_side_effects=True, vmem_limit_bytes=63 * 1024 * 1024
+            collective_id=0, has_side_effects=True, vmem_limit_bytes=38 * 1024 * 1024
         ),
         name="exchange",
     )(ao_rows, cot, cv)
 
 
-def _last_kernel(lhs_ref, g_ref, v_hbm, out_hbm, vbuf, rest, isem, osem):
+def _last_kernel(lhs_ref, g_ref, v_ref, out_hbm, vbuf, rest, osem):
     lane8 = lax.broadcasted_iota(jnp.int32, (8, LANES), 1)
 
-    def part(e, width, ref, into, sem):
+    def part(e, width):
         rows = pl.ds(pl.multiple_of(e * 16, 8), 8 * width)
-        src, dst = ref.at[:, rows, :], vbuf.at[:, rows, :]
-        return pltpu.make_async_copy(src, dst, sem.at[e]) if into else pltpu.make_async_copy(dst, src, sem.at[e])
-
-    for e in range(TILES // 2):
-        part(e, 2, v_hbm, True, isem).start()
-    part(TILES // 2, 1, v_hbm, True, isem).start()
+        return pltpu.make_async_copy(vbuf.at[:, rows, :], out_hbm.at[:, rows, :], osem.at[e])
 
     def put(e, width, tiles):
-        part(e, width, v_hbm, True, isem).wait()
         for w in range(width):
             rows = pl.ds(pl.multiple_of(e * 16 + 8 * w, 8), 8)
             for t in range(3):
-                vbuf[:, rows, t * LANES : (t + 1) * LANES] += tiles[3 * w + t]
-            vbuf[:, rows, 3 * LANES : PAIRS] += rest[:, rows, 0:REST]
-        part(e, width, out_hbm, False, osem).start()
+                vbuf[:, rows, t * LANES : (t + 1) * LANES] = v_ref[:, rows, t * LANES : (t + 1) * LANES] + tiles[3 * w + t]
+            vbuf[:, rows, 3 * LANES : PAIRS] = v_ref[:, rows, 3 * LANES : PAIRS] + rest[:, rows, 0:REST]
+        part(e, width).start()
 
     def load(g):
         return g_ref[:, pl.ds(pl.multiple_of(g * 16, 16), 16), :]
 
-    _step4(lhs_ref, load, put, rest, lane8)
+    _step4(lhs_ref, load, put, rest, lane8, True)
 
     for e in range(TILES // 2):
-        part(e, 2, out_hbm, False, osem).wait()
-    part(TILES // 2, 1, out_hbm, False, osem).wait()
+        part(e, 2).wait()
+    part(TILES // 2, 1).wait()
 
 
 def _last(lhs, g, v):
@@ -378,16 +348,15 @@
         in_specs=[
             pl.BlockSpec(memory_space=pltpu.VMEM),
             pl.BlockSpec(memory_space=pltpu.VMEM),
-            pl.BlockSpec(memory_space=pl.ANY),
+            pl.BlockSpec(memory_space=pltpu.VMEM),
         ],
         out_specs=pl.BlockSpec(memory_space=pl.ANY),
         scratch_shapes=[
             pltpu.VMEM((OCC, VIRT, PAIRS), F32),
             pltpu.VMEM((OCC, VIRT, LANES), F32),
             pltpu.SemaphoreType.DMA((TILES // 2 + 1,)),
-            pltpu.SemaphoreType.DMA((TILES // 2 + 1,)),
         ],
-        compiler_params=pltpu.CompilerParams(vmem_limit_bytes=50 * 1024 * 1024),
+        compiler_params=pltpu.CompilerParams(vmem_limit_bytes=30 * 1024 * 1024),
         name="last",
     )(lhs, g, v)
 

time: 170 us -> 164 us (0.965)
  Pallas kernels: 167 us -> 162 us
    pallas_call x1, Pallas kernels: 6.41 us -> 3.55 us  [_last(): pl.pallas_call(_last_kernel, out_shape=jax.ShapeDtypeStruct((OCC, VIRT, P...]
    pallas_call x1, Pallas kernels: 161 us -> 158 us  [_exchange(): pl.pallas_call(_exchange_kernel, out_shape=(jax.ShapeDtypeStruct((OCC, VI...]
where the time goes in v4:
time: 164 us; the launch traced here: 163 us
  Pallas kernels  162 us (99%)
    pallas_call x1, Pallas kernels, _exchange(): pl.pallas_call(_exchange_kernel, out_shape=(jax.ShapeDtypeStruct((OCC, VI...  158 us
    pallas_call x1, Pallas kernels, _last(): pl.pallas_call(_last_kernel, out_shape=jax.ShapeDtypeStruct((OCC, VIRT, P...  3.55 us

profile of v4, /device:TPU:0, one launch (start us, length us, event | category | flops | bytes accessed | tf_op | source)
XLA Modules:
  0.0 163.5 jit_solution(8227185709470166835)
XLA Ops:
  0.0 0.0 copy-start
  0.0 0.8 copy-done
  0.8 0.0 copy-start.1
  0.8 0.7 copy-done.1
  1.5 158.4 %exchange.1 = (f32[33,104,429]{2,1,0:T(8,128)S(1)}, bf16[16,352,128]{2,1,0:T(8,128)(2,1)S(1)}, bf16[528,256]{1,0:T(8,128)(2,1)S(1)}) custom-call(bf16[19,152,152,152]{3,2,1,0:T(8,128)(2,1)} %a_hbm.1, bf16[33,152]{1,0:T(8,128)(2,1)S(1)} %bitcast.1, bf16[152,104]{1,0:T(8,128)(2,1)S(1)} %copy-done), custom_call_target="tpu_custom_call" | custom-call | tf_op jit(solution)/shard_map/exchange/pallas_call | solution.py:288
  159.9 3.5 %last.1 = f32[33,104,429]{2,1,0:T(8,128)} custom-call(bf16[528,256]{1,0:T(8,128)(2,1)S(1)} %get-tuple-element.8.lhs_ref, bf16[16,352,128]{2,1,0:T(8,128)(2,1)S(1)} %get-tuple-element.9.g_ref, f32[33,104,429]{2,1,0:T(8,128)S(1)} %get-tuple-element.10.v_ref), custom_call_target="tpu_custom_call" | custom-call | tf_op jit(solution)/shard_map/last/pallas_call | solution.py:345
Async XLA Ops:
  0.0 0.8 copy-start
  0.8 0.7 copy-start.1

commit v5 on v4

--- a/solution.py
+++ b/solution.py
@@ -81,9 +81,9 @@
 
 
 def _exchange_kernel(
-    a_hbm, cot_ref, cv_ref, v_out, g_out, lhs_out,
+    a_hbm, cot_hbm, cv_hbm, v_out, g_out, lhs_out,
     abuf, cot, cvp, cvt, ts0, ts1, gsend, grecv, rest, lhs,
-    asem, ssem, rsem,
+    asem, ssem, rsem, csem, cot_ref, cv_ref,
 ):
     me = lax.axis_index("dev")
 
@@ -94,6 +94,10 @@
             asem.at[lax.rem(n, SLOTS)],
         )
 
+    cot_copy = pltpu.make_async_copy(cot_hbm, cot_ref, csem.at[0])
+    cv_copy = pltpu.make_async_copy(cv_hbm, cv_ref, csem.at[1])
+    cot_copy.start()
+    cv_copy.start()
     for n in range(SLOTS):
         a_copy(n).start()
 
@@ -103,6 +107,8 @@
             barrier, inc=1, device_id={"dev": lax.rem(me + k, DEVS)}, device_id_type=pl.DeviceIdType.MESH
         )
 
+    cot_copy.wait()
+    cv_copy.wait()
     cot[...] = jnp.zeros_like(cot)
     cot[0:OCC, :] = cot_ref[...]
     cvp[...] = jnp.zeros_like(cvp)
@@ -292,7 +298,7 @@
             jax.ShapeDtypeStruct((DEVS * LATE, BLK, LANES), BF16),
             jax.ShapeDtypeStruct((OCC * 16, DEVS * LATE * 16), BF16),
         ),
-        in_specs=[pl.BlockSpec(memory_space=pl.ANY)] + [pl.BlockSpec(memory_space=pltpu.VMEM)] * 2,
+        in_specs=[pl.BlockSpec(memory_space=pltpu.HBM)] * 3,
         out_specs=tuple(pl.BlockSpec(memory_space=pltpu.VMEM) for _ in range(3)),
         scratch_shapes=[
             pltpu.VMEM((SLOTS, CHUNK, AO, AO), BF16),
@@ -308,6 +314,9 @@
             pltpu.SemaphoreType.DMA((SLOTS,)),
             pltpu.SemaphoreType.DMA((ROWS, DEVS)),
             pltpu.SemaphoreType.DMA((ROWS, DEVS)),
+            pltpu.SemaphoreType.DMA((2,)),
+            pltpu.VMEM((OCC, AO), BF16),
+            pltpu.VMEM((AO, VIRT), BF16),
         ],
         compiler_params=pltpu.CompilerParams(
             collective_id=0, has_side_effects=True, vmem_limit_bytes=38 * 1024 * 1024
@@ -363,7 +372,7 @@
 
 def solution(mesh):
     def local_part(ao_rows, occ_coef, virt_coef):
-        v, g, lhs = _exchange(ao_rows, occ_coef.T, virt_coef)
+        v, g, lhs = _exchange(ao_rows, pltpu.with_memory_space_constraint(occ_coef.T, pltpu.HBM), pltpu.with_memory_space_constraint(virt_coef, pltpu.HBM))
         return _last(lhs, g, v)
 
     return jax.shard_map(

time: 164 us -> 164 us (level)
  no operation moved by 1% of the time
where the time goes in v5:
time: 164 us; the launch traced here: 163 us
  Pallas kernels  163 us (99%)
    pallas_call x1, Pallas kernels, _exchange(): pl.pallas_call(_exchange_kernel, out_shape=(jax.ShapeDtypeStruct((OCC, VI...  159 us
    pallas_call x1, Pallas kernels, _last(): pl.pallas_call(_last_kernel, out_shape=jax.ShapeDtypeStruct((OCC, VIRT, P...  3.54 us

profile of v5, /device:TPU:0, one launch (start us, length us, event | category | flops | bytes accessed | tf_op | source)
XLA Modules:
  0.0 162.7 jit_solution(7023267738815294514)
XLA Ops:
  0.0 159.1 %exchange.1 = (f32[33,104,429]{2,1,0:T(8,128)S(1)}, bf16[16,352,128]{2,1,0:T(8,128)(2,1)S(1)}, bf16[528,256]{1,0:T(8,128)(2,1)S(1)}) custom-call(bf16[19,152,152,152]{3,2,1,0:T(8,128)(2,1)} %a_hbm.1, bf16[33,152]{1,0:T(8,128)(2,1)} %bitcast.1, bf16[152,104]{1,0:T(8,128)(2,1)} %cv_hbm.1), custom_call_target="tpu_custom_call" | custom-call | tf_op jit(solution)/shard_map/exchange/pallas_call | solution.py:294
  159.2 3.5 %last.1 = f32[33,104,429]{2,1,0:T(8,128)} custom-call(bf16[528,256]{1,0:T(8,128)(2,1)S(1)} %get-tuple-element.8.lhs_ref, bf16[16,352,128]{2,1,0:T(8,128)(2,1)S(1)} %get-tuple-element.9.g_ref, f32[33,104,429]{2,1,0:T(8,128)S(1)} %get-tuple-element.10.v_ref), custom_call_target="tpu_custom_call" | custom-call | tf_op jit(solution)/shard_map/last/pallas_call | solution.py:354

commit v6 on v5

--- a/solution.py
+++ b/solution.py
@@ -13,7 +13,7 @@
 DEVS = 8
 ROWS = AO // DEVS
 PAIRS = OCC * VIRT // DEVS
-PITCH = 40
+PITCH = 41
 CHUNK = 19
 CHUNKS = AO // CHUNK
 SLOTS = 4
@@ -24,6 +24,7 @@
 RTILES = -(-TILES * REST // LANES)
 BLK = 8 * (3 * TILES + RTILES)
 GROUPS = ((0, 1, 2, 3, 4, 5), (6, 7, 8, 9, 10, 11, 12, 13), (14, 15, 16, 17, 18, 19, 20, 21), (22, 23, 24, 25, 26, 27, 28, 29, 30, 31, 32))
+ORDER = (0, 2, 4, 6, 1, 3, 5, 7)
 EARLY = 17
 LATE = ROWS - EARLY
 
@@ -170,9 +171,9 @@
             a_copy(n).wait()
             for u in range(CHUNK):
                 t = jnp.dot(cot[...], abuf[slot, u], preferred_element_type=F32)
-                base = pl.multiple_of((c * CHUNK + u) * PITCH, 8)
-                ts0[pl.ds(base, PITCH), :] = t[:, 0:LANES]
-                ts1[pl.ds(base, PITCH), 0 : AO - LANES] = t[:, LANES:AO]
+                base = (c * CHUNK + u) * PITCH
+                ts0[pl.ds(base, 40), :] = t[:, 0:LANES]
+                ts1[pl.ds(base, 40), 0 : AO - LANES] = t[:, LANES:AO]
 
             @pl.when(n + SLOTS < ROWS * CHUNKS)
             def _():
@@ -211,7 +212,7 @@
             for n, jj in enumerate(group):
                 g[jj] = full[:, LANES * n : LANES * n + LANES]
 
-        for d in range(DEVS):
+        for at, d in enumerate(ORDER):
             first = PAIRS * d
             j0, j1 = first // VIRT, (first + PAIRS - 1) // VIRT
             rolled = {}
@@ -242,9 +243,9 @@
                     part = jnp.where(lane8 >= REST * n - LANES * k, moved[n], part)
                 parts.append(part)
             gsend[lax.rem(row, RING), d] = jnp.concatenate(parts, axis=0).astype(BF16)
-            if d:
-                send(row, d - 1)
-        send(row, DEVS - 1)
+            if at:
+                send(row, ORDER[at - 1])
+        send(row, ORDER[-1])
         return carry
 
     lax.fori_loop(0, ROWS, row_body, 0)
@@ -302,7 +303,7 @@
         out_specs=tuple(pl.BlockSpec(memory_space=pltpu.VMEM) for _ in range(3)),
         scratch_shapes=[
             pltpu.VMEM((SLOTS, CHUNK, AO, AO), BF16),
-            pltpu.VMEM((PITCH, AO), BF16),
+            pltpu.VMEM((40, AO), BF16),
             pltpu.VMEM((AO, LANES), BF16),
             pltpu.VMEM((VIRT, AO), BF16),
             pltpu.VMEM((AO * PITCH, LANES), F32),

time: 164 us -> 163 us (level)
  no operation moved by 1% of the time
where the time goes in v6:
time: 163 us; the launch traced here: 162 us
  Pallas kernels  162 us (99%)
    pallas_call x1, Pallas kernels, _exchange(): pl.pallas_call(_exchange_kernel, out_shape=(jax.ShapeDtypeStruct((OCC, VI...  158 us
    pallas_call x1, Pallas kernels, _last(): pl.pallas_call(_last_kernel, out_shape=jax.ShapeDtypeStruct((OCC, VIRT, P...  3.54 us

profile of v6, /device:TPU:0, one launch (start us, length us, event | category | flops | bytes accessed | tf_op | source)
XLA Modules:
  0.0 161.7 jit_solution(6289982123085728775)
XLA Ops:
  0.0 158.1 %exchange.1 = (f32[33,104,429]{2,1,0:T(8,128)S(1)}, bf16[16,352,128]{2,1,0:T(8,128)(2,1)S(1)}, bf16[528,256]{1,0:T(8,128)(2,1)S(1)}) custom-call(bf16[19,152,152,152]{3,2,1,0:T(8,128)(2,1)} %a_hbm.1, bf16[33,152]{1,0:T(8,128)(2,1)} %bitcast.1, bf16[152,104]{1,0:T(8,128)(2,1)} %cv_hbm.1), custom_call_target="tpu_custom_call" | custom-call | tf_op jit(solution)/shard_map/exchange/pallas_call | solution.py:295
  158.1 3.5 %last.1 = f32[33,104,429]{2,1,0:T(8,128)} custom-call(bf16[528,256]{1,0:T(8,128)(2,1)S(1)} %get-tuple-element.8.lhs_ref, bf16[16,352,128]{2,1,0:T(8,128)(2,1)S(1)} %get-tuple-element.9.g_ref, f32[33,104,429]{2,1,0:T(8,128)S(1)} %get-tuple-element.10.v_ref), custom_call_target="tpu_custom_call" | custom-call | tf_op jit(solution)/shard_map/last/pallas_call | solution.py:355
